TPU v7x, 32 devices: a whole 2x2x4 slice. The times are simulated.
32 devices in a mesh: rep: 2 (over y), dp: 16 (over z, x, core).
Axes of the slice: x: 2, y: 2, z: 4, core: 2. Of those that a mesh axis runs over, the one named last changes fastest.
Arguments:
- hidden: bfloat16 [256, 2, 3584], P(('rep', 'dp')), may hold values from -96 to 96
- lm_head: bfloat16 [3584, 12288], P(None, ('rep', 'dp')), may hold values from -0.3125 to 0.3125
- reward_head: bfloat16 [3584], replicated, may hold values from -0.09375 to 0.09375
- target_ids: int32 [256, 2], P(('rep', 'dp')), may hold values from 0 to 12287
- lengths: int32 [256], P(('rep', 'dp')), may hold values from 1 to 2
- prompt_ids: int32 [256], P(('rep', 'dp')), may hold values from 0 to 15, as said below
Outputs:
- token_logprobs: float32 [256, 2], P(('rep', 'dp'))
- advantages: float32 [256], P(('rep', 'dp'))
Inputs may be any that keep to these rules, and one draw needn't show every extreme that they name: `prompt_ids`: each prompt id names exactly 16 responses.
All inputs are finite; a program needn't handle non-finite values.
Results may differ from a plain program's by a relative error of at most 0.0003.
Values may be sent and summed in bfloat16 or wider, within the bound.
No kernel may reach another device: no remote copies, remote signals or barrier semaphores. Data moves between devices by JAX's collectives and lax.ppermute only.
A program may use at most 128 MiB of HBM per device.

v0:
```python
import jax
import jax.numpy as jnp
from jax import lax
from jax.sharding import PartitionSpec as P

GROUP = 16
PROM_DEV = 1


def moments(stacked):
    means = stacked[0] / GROUP
    scales = jnp.sqrt(jnp.maximum(stacked[1] / GROUP - means * means, 1.0))
    return (means, scales)


def local(hidden, lm_head, reward_head, target_ids, lengths, prompt_ids):
    resp_dev, window, width = hidden.shape
    voc_dev = lm_head.shape[1]
    owners = lax.axis_size("dp")
    me = lax.axis_index("rep") * owners + lax.axis_index("dp")
    tok_dev = resp_dev * window
    all_ids = lax.all_gather(target_ids.reshape(tok_dev), ("rep", "dp"), axis=0, tiled=True)
    local_ids = all_ids - me * voc_dev
    columns = lax.broadcasted_iota(jnp.int32, (1, voc_dev), 1)
    piece = lax.all_gather(hidden, ("rep", "dp"), axis=0, tiled=True)
    count = piece.shape[0] * window
    flat = piece.reshape(count, width)
    logits = jnp.dot(flat, lm_head, preferred_element_type=jnp.float32)
    peak = jnp.max(logits, axis=1)
    total = jnp.sum(jnp.exp(logits - peak[:, None]), axis=1)
    picked = jnp.sum(jnp.where(columns == local_ids[:, None], logits, 0.0), axis=1)
    totals = total
    picks = picked
    first_own = me * tok_dev
    whole_top = lax.pmax(peak, ("rep", "dp"))
    scaled = totals * jnp.exp(peak - whole_top)
    whole_total, whole_pick = lax.psum((scaled, picks), ("rep", "dp"))
    top = lax.dynamic_slice_in_dim(whole_top, first_own, tok_dev)
    total = lax.dynamic_slice_in_dim(whole_total, first_own, tok_dev)
    picked = lax.dynamic_slice_in_dim(whole_pick, first_own, tok_dev)
    logprob = (picked - (top + jnp.log(total))).reshape(resp_dev, window)
    positions = lax.broadcasted_iota(jnp.int32, (resp_dev, window), 1)
    token_logprobs = jnp.where(positions < lengths[:, None], logprob, 0.0)
    last = jnp.take_along_axis(hidden, (lengths - 1)[:, None, None], axis=1)[:, 0, :]
    rewards = jnp.dot(last, reward_head, preferred_element_type=jnp.float32)
    prompts = PROM_DEV * owners
    member = (prompt_ids[:, None] == lax.broadcasted_iota(jnp.int32, (1, prompts), 1)).astype(
        jnp.float32
    )
    sums = jnp.dot(rewards, member, precision=lax.Precision.HIGHEST)
    squares = jnp.dot(rewards * rewards, member, precision=lax.Precision.HIGHEST)
    stacked = jnp.stack([sums, squares])
    whole = lax.psum(stacked, ("rep", "dp"))
    means, scales = moments(whole)
    centre = jnp.dot(member, means, precision=lax.Precision.HIGHEST)
    spread = jnp.dot(member, scales, precision=lax.Precision.HIGHEST)
    advantages = (rewards - centre) / spread
    return (token_logprobs, advantages)


def solution(mesh):
    in_specs = (
        P(("rep", "dp"), None, None),
        P(None, ("rep", "dp")),
        P(),
        P(("rep", "dp"), None),
        P(("rep", "dp")),
        P(("rep", "dp")),
    )
    out_specs = (P(("rep", "dp"), None), P(("rep", "dp")))
    return jax.shard_map(local, mesh=mesh, in_specs=in_specs, out_specs=out_specs, check_vma=False)
```

profile of v0, /device:TPU:0, one launch (start us, length us, event | category | flops | bytes accessed | tf_op | source)
XLA Modules:
  0.0 176.3 jit_solution(201014197052093637)
XLA Ops:
  7.2 0.0 copy-start
  7.2 0.0 all-gather.2.cloned.1.call-start
  7.2 0.7 all-gather.2.cloned.1.call-update
  7.9 0.8 copy.12
  8.8 0.1 reshape.52
  8.8 0.7 reshape.54
  9.5 0.7 fusion.27
  10.2 1.6 gather_fusion
  11.8 0.2 dynamic-update-slice
  12.0 42.1 %all-reduce = s32[512]{0:T(512)S(1)} all-reduce(s32[512]{0:T(512)S(1)} %dynamic-update-slice), channel_id=1, replica_groups=mesh['rep'=2,'dp'=16] {'rep','dp'}, use_global_device_ids=true, to_apply=%add | all-reduce | flops 512 | bytes 4096
  54.1 0.7 compare_and_fusion
  54.8 0.2 fusion.2
  55.0 0.0 copy-start.1
  55.0 0.9 fusion.6
  55.8 0.9 fusion.7
  56.7 0.6 pad_maximum_fusion
  57.3 0.0 copy-done.1
  57.3 17.1 %all-gather.2.cloned.1.call-done = bf16[256,2,3584]{2,1,0:T(2,128)(2,1)} async-done(((bf16[8,2,3584]{2,1,0:T(2,128)(2,1)}), bf16[256,2,3584]{2,1,0:T(2,128)(2,1)}) %all-gather.2.cloned.1.call-update) | async-done | bytes 3670032 | tf_op jit(solution)/shard_map/all_gather | solution.py:25
  74.4 8.4 %reshape.41 = bf16[512,3584]{1,0:T(8,128)(2,1)} reshape(bf16[256,2,3584]{2,1,0:T(2,128)(2,1)} %all-gather.2.cloned.1.call-done) | data formatting | bytes 7340032 | tf_op jit(solution)/shard_map/reshape | solution.py:27
  82.8 0.0 copy-done
  82.8 3.7 %fusion.28 = (f32[512]{0:T(512)S(1)}, f32[512,384]{0,1:T(8,128)S(1)}) fusion(bf16[512,3584]{1,0:T(8,128)(2,1)} %reshape.41, bf16[3584,384]{1,0:T(8,128)(2,1)S(1)} %copy-done), kind=kOutput, calls=%fused_computation.46 | convolution fusion | flops 1409482240 | bytes 7211008 | tf_op jit(solution)/shard_map/dot_general | solution.py:28
  86.4 38.2 %pmax.7 = f32[512]{0:T(512)S(1)} all-reduce(f32[512]{0:T(512)S(1)} %get-tuple-element.13), channel_id=1, replica_groups=mesh['rep'=2,'dp'=16] {'rep','dp'}, use_global_device_ids=true, to_apply=%region_3.4 | all-reduce | flops 512 | bytes 4096 | tf_op jit(solution)/shard_map/pmax | solution.py:35
  124.7 0.2 select_reduce_fusion
  124.9 40.7 %all-reduce.1 = (f32[512]{0:T(512)S(1)}, f32[512]{0:T(512)S(1)}, f32[2,16]{1,0:T(2,128)S(1)}) all-reduce(f32[512]{0:T(512)S(1)} %exponential_multiply_fusion, f32[512]{0:T(512)S(1)} %get-tuple-element.8, f32[2,16]{1,0:T(2,128)} %pad_maximum_fusion), channel_id=1, replica_groups=mesh['rep'=2,'dp'=16] {'rep','dp'}, use_global_device_ids=true, to_apply=%region_5.6 | all-reduce | flops 1056 | bytes 8448 | tf_op jit(solution)/shard_map/psum | solution.py:37
  165.7 0.1 add_subtract_fusion
  165.8 0.1 reshape.42
  165.8 0.7 fusion.8
  166.6 0.6 copy.13
  167.2 0.8 convolution_bitcast_fusion
  168.0 1.4 fusion.1
  (6 shorter events, 0.0 us)
Async XLA Ops:
  7.2 75.6 %copy-start = (bf16[3584,384]{1,0:T(8,128)(2,1)S(1)}, bf16[3584,384]{1,0:T(8,128)(2,1)}, u32[]{:S(2)}) copy-start(bf16[3584,384]{1,0:T(8,128)(2,1)} %param.7) | copy-start | bytes 8257540
  7.2 67.2 %all-gather.2.cloned.1.call-start = ((), (), s32[]{:S(2)}) async-start(), calls=%async_computation | async-start | bytes 3784704 | tf_op jit(solution)/shard_map/all_gather | solution.py:25
  55.0 2.3 %copy-start.1 = (f32[1,8]{1,0:T(1,128)}, f32[1,8]{1,0:T(1,128)S(1)}, u32[]{:S(2)}) copy-start(f32[1,8]{1,0:T(1,128)S(1)} %fusion.2) | copy-start | bytes 100
Sparse Core Ops, SparseCore 0:
  10.8 63.4 all-gather.1
where the time goes:
time: 177 us; the launch traced here: 176 us
  blocking collectives  121 us (68%)
  waiting for transfers between devices  17.7 us (10%)
  between operations  14.1 us (8%)
  local copies, waits for them, and re-layouts  12.6 us (7%)
  matrix products  7.85 us (4%)
  other arithmetic  2.97 us (2%)
    unnamed x1, blocking collectives  42.1 us
    psum x1, blocking collectives, local(): whole_total, whole_pick = lax.psum((scaled, picks), ('rep', 'dp'))  40.7 us
    pmax x1, blocking collectives, local(): whole_top = lax.pmax(peak, ('rep', 'dp'))  38.2 us
    all_gather x1, waiting for transfers between devices, local(): piece = lax.all_gather(hidden, ('rep', 'dp'), axis=0, tiled=True)  17.1 us
    reshape x1, local copies, waits for them, and re-layouts, local(): flat = piece.reshape(count, width)  8.4 us
    dot_general x1, matrix products, local(): logits = jnp.dot(flat, lm_head, preferred_element_type=jnp.float32)  3.68 us
  transfers between devices with their start and end apart: 1, of which 1 were waited for; matrix products, arithmetic and copies ran while one was open for 4% of the time, Pallas kernels for 0%

commit v1 on v0

--- a/solution.py
+++ b/solution.py
@@ -5,6 +5,11 @@
 
 GROUP = 16
 PROM_DEV = 1
+
+
+def axis_by_axis(array, one, other):
+    partial = lax.psum(array, one)
+    return lax.psum(partial, other)
 
 
 def moments(stacked):
@@ -34,7 +39,7 @@
     first_own = me * tok_dev
     whole_top = lax.pmax(peak, ("rep", "dp"))
     scaled = totals * jnp.exp(peak - whole_top)
-    whole_total, whole_pick = lax.psum((scaled, picks), ("rep", "dp"))
+    whole_total, whole_pick = axis_by_axis((scaled, picks), "dp", "rep")
     top = lax.dynamic_slice_in_dim(whole_top, first_own, tok_dev)
     total = lax.dynamic_slice_in_dim(whole_total, first_own, tok_dev)
     picked = lax.dynamic_slice_in_dim(whole_pick, first_own, tok_dev)

time: 177 us -> 197 us (1.11)
  blocking collectives: 121 us -> 158 us
  waiting for transfers between devices: 17.7 us -> 0.68 us
    psum x1 -> x3, blocking collectives: 40.7 us -> 78.2 us  [the longest x1 42.1 us: local(): whole = lax.psum(stacked, ('rep', 'dp'))]
    all_gather x1, waiting for transfers between devices: 17.1 us -> 0.01 us  [local(): piece = lax.all_gather(hidden, ('rep', 'dp'), axis=0, tiled=True)]
    unnamed x1, blocking collectives: 42.1 us -> 40.1 us
  transfers between devices with their start and end apart: 1 -> 1, of which waited for: 1 -> 0; matrix products, arithmetic and copies ran while one was open for 4% -> 5% of each run, Pallas kernels for 0% -> 0%
where the time goes in v1:
time: 197 us; the launch traced here: 196 us
  blocking collectives  158 us (80%)
  between operations  14.1 us (7%)
  local copies, waits for them, and re-layouts  12.5 us (6%)
  matrix products  7.79 us (4%)
  other arithmetic  2.41 us (1%)
    psum x1, blocking collectives, local(): whole = lax.psum(stacked, ('rep', 'dp'))  42.1 us
    unnamed x1, blocking collectives  40.1 us
    pmax x1, blocking collectives, local(): whole_top = lax.pmax(peak, ('rep', 'dp'))  40 us
    psum x1, blocking collectives, axis_by_axis(): partial = lax.psum(array, one)  31.1 us
    reshape x1, local copies, waits for them, and re-layouts, local(): flat = piece.reshape(count, width)  8.4 us
    psum x1, blocking collectives, axis_by_axis(): return lax.psum(partial, other)  4.91 us
  transfers between devices with their start and end apart: 1, of which 0 were waited for; matrix products, arithmetic and copies ran while one was open for 5% of the time, Pallas kernels for 0%

profile of v1, /device:TPU:0, one launch (start us, length us, event | category | flops | bytes accessed | tf_op | source)
XLA Modules:
  0.0 195.8 jit_solution(4325485700644569284)
XLA Ops:
  7.2 0.0 copy-start
  7.2 0.0 all-gather.2.cloned.1.call-start
  7.2 0.7 all-gather.2.cloned.1.call-update
  7.9 0.8 reshape.54
  8.7 0.7 fusion.27
  9.4 1.6 gather_fusion
  11.0 0.7 compare_and_fusion
  11.6 0.2 fusion.2
  11.8 0.9 fusion.6
  12.7 0.8 fusion.7
  13.5 42.1 %psum.39 = f32[2,16]{1,0:T(2,128)S(1)} all-reduce(f32[2,16]{1,0:T(2,128)S(1)} %pad_maximum_fusion), channel_id=1, replica_groups=mesh['rep'=2,'dp'=16] {'rep','dp'}, use_global_device_ids=true, to_apply=%region_8.9 | all-reduce | flops 32 | bytes 256 | tf_op jit(solution)/shard_map/psum | solution.py:58
  55.7 0.8 copy.12
  56.4 0.1 reshape.52
  56.5 0.2 dynamic-update-slice
  56.7 40.1 %all-reduce = s32[512]{0:T(512)S(1)} all-reduce(s32[512]{0:T(512)S(1)} %dynamic-update-slice), channel_id=1, replica_groups=mesh['rep'=2,'dp'=16] {'rep','dp'}, use_global_device_ids=true, to_apply=%add | all-reduce | flops 512 | bytes 4096
  96.8 0.8 convolution_bitcast_fusion
  97.6 1.4 fusion.1
  99.0 0.0 all-gather.2.cloned.1.call-done
  99.0 8.4 %reshape.41 = bf16[512,3584]{1,0:T(8,128)(2,1)} reshape(bf16[256,2,3584]{2,1,0:T(2,128)(2,1)} %all-gather.2.cloned.1.call-done) | data formatting | bytes 7340032 | tf_op jit(solution)/shard_map/reshape | solution.py:32
  107.4 0.0 copy-done
  107.4 3.7 %fusion.28 = (f32[512]{0:T(512)S(1)}, f32[512,384]{0,1:T(8,128)S(1)}) fusion(bf16[512,3584]{1,0:T(8,128)(2,1)} %reshape.41, bf16[3584,384]{1,0:T(8,128)(2,1)S(1)} %copy-done), kind=kOutput, calls=%fused_computation.46 | convolution fusion | flops 1409482240 | bytes 7211008 | tf_op jit(solution)/shard_map/dot_general | solution.py:33
  111.1 40.0 %pmax.7 = f32[512]{0:T(512)S(1)} all-reduce(f32[512]{0:T(512)S(1)} %get-tuple-element.14), channel_id=1, replica_groups=mesh['rep'=2,'dp'=16] {'rep','dp'}, use_global_device_ids=true, to_apply=%region_4.5 | all-reduce | flops 512 | bytes 4096 | tf_op jit(solution)/shard_map/pmax | solution.py:40
  151.1 0.2 select_reduce_fusion
  151.4 31.1 %all-reduce.1 = (f32[512]{0:T(512)S(1)}, f32[512]{0:T(512)S(1)}) all-reduce(f32[512]{0:T(512)S(1)} %exponential_multiply_fusion, f32[512]{0:T(512)S(1)} %get-tuple-element.8), channel_id=1, replica_groups=mesh['rep'=2,'dp'=16] {'dp'}, use_global_device_ids=true, to_apply=%region_6.7 | all-reduce | flops 1024 | bytes 8192 | tf_op jit(solution)/shard_map/psum | solution.py:11
  182.5 4.9 %all-reduce.2 = (f32[512]{0:T(512)S(1)}, f32[512]{0:T(512)S(1)}) all-reduce(f32[512]{0:T(512)S(1)} %get-tuple-element.10, f32[512]{0:T(512)S(1)} %get-tuple-element.11), channel_id=1, replica_groups=mesh['rep'=2,'dp'=16] {'rep'}, use_global_device_ids=true, to_apply=%region_7.8 | all-reduce | flops 1024 | bytes 8192 | tf_op jit(solution)/shard_map/psum | solution.py:12
  187.4 0.1 add_subtract_fusion
  187.5 0.1 reshape.42
  187.6 0.7 fusion.8
  188.3 0.6 copy.13
  (7 shorter events, 0.0 us)
Async XLA Ops:
  7.2 100.2 %copy-start = (bf16[3584,384]{1,0:T(8,128)(2,1)S(1)}, bf16[3584,384]{1,0:T(8,128)(2,1)}, u32[]{:S(2)}) copy-start(bf16[3584,384]{1,0:T(8,128)(2,1)} %param.7) | copy-start | bytes 8257540
  7.2 91.8 %all-gather.2.cloned.1.call-start = ((), (), s32[]{:S(2)}) async-start(), calls=%async_computation | async-start | bytes 3784704 | tf_op jit(solution)/shard_map/all_gather | solution.py:30
Sparse Core Ops, SparseCore 0:
  10.8 63.0 all-gather.1
